TPU v7x, 32 devices: a whole 2x2x4 slice. The times are simulated.
32 devices in a mesh: dp: 4 (over y, x), expert: 4 (over z), mp: 2 (over core).
Axes of the slice: x: 2, y: 2, z: 4, core: 2. Of those that a mesh axis runs over, the one named last changes fastest.
Arguments:
- base_weights: bfloat16 [8, 2560, 3072], P('expert', None, 'mp'), may hold values from -6 to 6
- delta_blocks: bfloat16 [512, 128, 128], P(('dp', 'expert', 'mp')), may hold values from -4 to 4
- block_ids: int32 [512], P(('dp', 'expert', 'mp')), may hold values from 0 to 3839, as said below
- block_counts: int32 [256], P(('dp', 'expert', 'mp')), may hold values from 0 to 2, as said below
- owner_map: int32 [8], replicated, may hold values from 0 to 7, as said below
Outputs:
- merged_weights: bfloat16 [8, 2560, 3072], P('expert', None, 'mp')
Inputs may be any that keep to these rules, and one draw needn't show every extreme that they name: A permutation: expert e is held in serving position owner_map[e], by the serving group owner_map[e] // 2. `block_ids`: every slot of device s for owner q, used or not, names a block (e * 20 + r) * 24 + c with owner_map[e] // 2 == q // 2 and c // 12 == q % 2. Names may repeat within and across devices. `block_counts`: at most 2 used slots from one device to one owner; in every draw some owner receives exactly 2 blocks from every device.
All inputs are finite; a program needn't handle non-finite values.
Results may differ from a plain program's by a relative error of at most 0.001.
Values may be sent and summed in bfloat16 or wider, within the bound.
A program may use at most 192 MiB of HBM per device.

v0:
```python
import jax
import jax.numpy as jnp
from jax import lax
from jax.sharding import PartitionSpec as P


def to_matrix(summed, exp_dev, row_blocks, col_blocks, block_size):
    grid = summed.reshape(exp_dev, row_blocks, col_blocks, block_size, block_size)
    return grid.transpose(0, 1, 3, 2, 4).reshape(
        exp_dev, row_blocks * block_size, col_blocks * block_size
    )


def body(base_weights, delta_blocks, block_ids, block_counts, owner_map):
    exp_dev, row_count, col_count = base_weights.shape
    block_size = delta_blocks.shape[1]
    row_blocks = row_count // block_size
    col_blocks = col_count // block_size
    col_total = col_blocks * lax.axis_size("mp")
    slot_total = delta_blocks.shape[0]
    capacity = slot_total // block_counts.shape[0]
    active = jnp.arange(slot_total, dtype=jnp.int32) % capacity < jnp.repeat(block_counts, capacity)
    values = jnp.where(active[:, None, None], delta_blocks, jnp.zeros((), jnp.bfloat16))
    expert = block_ids // (row_blocks * col_total)
    remain = block_ids % (row_blocks * col_total)
    row_index = remain // col_total
    col_index = remain % col_total
    expert_count = owner_map.shape[0]
    matches = expert[:, None] == jnp.arange(expert_count, dtype=jnp.int32)[None, :]
    position = jnp.sum(jnp.where(matches, owner_map[None, :], 0), axis=1)
    idents = (position % exp_dev * row_blocks + row_index) * col_blocks + col_index % col_blocks
    arrived = lax.all_to_all(values, ("expert", "mp"), split_axis=0, concat_axis=0, tiled=True)
    arrived_ids = lax.all_to_all(idents, ("expert", "mp"), split_axis=0, concat_axis=0, tiled=True)
    empty = jnp.zeros((exp_dev * row_blocks * col_blocks, block_size, block_size), jnp.float32)
    every_ids = lax.all_gather(arrived_ids, "dp", axis=0, tiled=True)
    summed = empty.at[every_ids].add(
        lax.all_gather(arrived, "dp", axis=0, tiled=True).astype(jnp.float32)
    )
    task_delta = to_matrix(summed, exp_dev, row_blocks, col_blocks, block_size)
    return (base_weights.astype(jnp.float32) + task_delta).astype(jnp.bfloat16)


def solution(mesh):
    in_specs = (
        P("expert", None, "mp"),
        P(("dp", "expert", "mp"), None, None),
        P(("dp", "expert", "mp")),
        P(("dp", "expert", "mp")),
        P(),
    )
    out_specs = P("expert", None, "mp")
    return jax.shard_map(body, mesh=mesh, in_specs=in_specs, out_specs=out_specs, check_vma=False)
```

profile of v0, /device:TPU:0, one launch (start us, length us, event | category | flops | bytes accessed | tf_op | source)
XLA Modules:
  0.0 217.0 jit_solution(12489329128160570019)
XLA Ops:
  6.5 0.7 broadcast_in_dim.41
  7.3 0.1 reshape.27
  7.4 1.1 broadcast_select_fusion
  8.5 21.6 %all_to_all.17 = bf16[16,128,128]{2,1,0:T(8,128)(2,1)} all-to-all(bf16[16,128,128]{2,1,0:T(8,128)(2,1)S(1)} %broadcast_select_fusion), channel_id=1, replica_groups=mesh['dp'=4,'expert'=4,'mp'=2] {'expert','mp'}, dimensions={0} | all-to-all | bytes 1048576 | tf_op jit(solution)/shard_map/all_to_all | solution.py:32
  30.1 0.0 all-gather.2.cloned.1.call-update
  30.1 0.7 and_select_fusion.6
  30.8 0.7 select_reduce_fusion
  31.5 0.7 fusion
  32.2 0.7 all_to_all.11
  32.9 3.3 %all-to-all-start = ((s32[8,2,1]{1,2,0:T(1,128)}), s32[8,2,1]{1,2,0:T(1,128)S(1)}, u32[]{:S(2)}, u32[]{:S(2)}) async-start(s32[8,2,1]{1,2,0:T(1,128)} %bitcast), calls=%async_computation | async-start | bytes 8192 | tf_op jit(solution)/shard_map/all_to_all | solution.py:33
  36.2 20.7 %copy.13 = bf16[2,2560,1536]{1,2,0:T(8,128)(2,1)} copy(bf16[2,2560,1536]{2,1,0:T(8,128)(2,1)} %param.5) | data formatting | bytes 31457280 | tf_op args[0]
  57.0 0.6 dynamic-slice
  58.1 0.6 broadcast.52
  58.7 0.7 reduce.3
  59.5 0.1 reshape.39
  59.5 0.2 dynamic-update-slice
  59.8 7.3 %all-reduce = s32[64]{0:T(128)S(1)} all-reduce(s32[64]{0:T(128)S(1)} %dynamic-update-slice), channel_id=1, replica_groups=mesh['dp'=4,'expert'=4,'mp'=2] {'dp'}, use_global_device_ids=true, to_apply=%add | all-reduce | flops 64 | bytes 512
  67.0 4.0 %convert_element_type.10 = f32[64,128,128]{2,1,0:T(8,128)} convert(bf16[64,128,128]{2,1,0:T(8,128)(2,1)} %all-gather.2.cloned.1.call-done) | non-fusion elementwise | flops 1048576 | bytes 6291456 | tf_op jit(solution)/shard_map/convert_element_type | solution.py:37
  71.1 14.4 %broadcast_in_dim.37 = f32[480,128,128]{2,1,0:T(8,128)} broadcast(f32[]{:T(128)} %constant.56.clone.1), dimensions={} | broadcast | bytes 31457284 | tf_op jit(solution)/shard_map/broadcast_in_dim | solution.py:34
  85.5 13.7 %scatter_fusion = f32[480,128,128]{2,1,0:T(8,128)} fusion(f32[480,128,128]{2,1,0:T(8,128)} %broadcast_in_dim.37, s32[64]{0:T(128)S(1)} %compare_select_fusion, f32[64,128,128]{2,1,0:T(8,128)} %convert_element_type.10), kind=kCustom, calls=%fused_computation | custom fusion | flops 1048576 | bytes 12583168 | tf_op jit(solution)/shard_map/scatter-add | solution.py:36
  99.2 34.3 %copy.15 = f32[2,20,128,12,128]{2,1,4,3,0:T(8,128)} copy(f32[2,20,128,12,128]{4,2,3,1,0:T(8,128)} %bitcast.8) | data formatting | bytes 62914560 | tf_op jit(solution)/shard_map/transpose | solution.py:9
  133.4 35.5 %reshape.29 = f32[2,2560,1536]{1,2,0:T(8,128)} reshape(f32[2,20,128,12,128]{2,1,4,3,0:T(8,128)} %copy.15) | data formatting | bytes 62914560 | tf_op jit(solution)/shard_map/reshape | solution.py:9
  168.9 20.7 %add_convert_fusion = bf16[2,2560,1536]{1,2,0:T(8,128)(2,1)} fusion(f32[2,2560,1536]{1,2,0:T(8,128)} %reshape.29, bf16[2,2560,1536]{1,2,0:T(8,128)(2,1)} %copy.13), kind=kLoop, calls=%fused_computation.1 | loop fusion | flops 23592960 | bytes 62914560 | tf_op jit(solution)/shard_map/convert_element_type | solution.py:40
  189.6 20.6 %copy.16 = bf16[2,2560,1536]{2,1,0:T(8,128)(2,1)} copy(bf16[2,2560,1536]{1,2,0:T(8,128)(2,1)} %add_convert_fusion) | data formatting | bytes 31457280 | tf_op jit(solution)/shard_map/convert_element_type | solution.py:40
  (8 shorter events, 0.0 us)
Async XLA Ops:
  6.5 60.5 %all-gather.2.cloned.1.call-start = ((), (), s32[]{:S(2)}) async-start(), calls=%async_computation.2 | async-start | bytes 2621440 | tf_op jit(solution)/shard_map/all_gather | solution.py:37
  32.9 25.2 %all-to-all-start = ((s32[8,2,1]{1,2,0:T(1,128)}), s32[8,2,1]{1,2,0:T(1,128)S(1)}, u32[]{:S(2)}, u32[]{:S(2)}) async-start(s32[8,2,1]{1,2,0:T(1,128)} %bitcast), calls=%async_computation | async-start | bytes 8192 | tf_op jit(solution)/shard_map/all_to_all | solution.py:33
  36.2 20.7 %copy-start = (u32[32]{0:T(128)S(1)}, u32[32]{0:T(128)}, u32[]{:S(2)}) copy-start(u32[32]{0:T(128)} %constant.72) | copy-start | bytes 388
Sparse Core Ops, SparseCore 0:
  30.2 34.1 all-gather.1
where the time goes:
time: 220 us; the launch traced here: 217 us
  local copies, waits for them, and re-layouts  128 us (58%)
  other arithmetic  42.4 us (19%)
  blocking collectives  28.8 us (13%)
  between operations  14 us (6%)
  starting transfers between devices  3.34 us (2%)
    reshape x1, local copies, waits for them, and re-layouts, to_matrix(): grid.transpose(0, 1, 3, 2, 4)  35.5 us
    transpose x1, local copies, waits for them, and re-layouts, to_matrix(): grid.transpose(0, 1, 3, 2, 4)  34.3 us
    all_to_all x1, blocking collectives, body(): lax.all_to_all(values, ('expert', 'mp'), split_axis=0, concat_axis=0, til...  21.6 us
    unnamed x6, local copies, waits for them, and re-layouts  21.5 us
    convert_element_type x1, other arithmetic, body(): return (base_weights.astype(jnp.float32) + task_delta).astype(jnp.bfloat16)  20.7 us
    convert_element_type x1, local copies, waits for them, and re-layouts, body(): return (base_weights.astype(jnp.float32) + task_delta).astype(jnp.bfloat16)  20.6 us
    broadcast_in_dim x1, local copies, waits for them, and re-layouts, body(): jnp.zeros((exp_dev * row_blocks * col_blocks, block_size, block_size), jn...  14.4 us
    scatter-add x1, other arithmetic, body(): empty.at[every_ids]  13.7 us
  transfers between devices with their start and end apart: 2, of which 0 were waited for; matrix products, arithmetic and copies ran while one was open for 12% of the time, Pallas kernels for 0%

commit v1 on v0

v1 whole, which is shorter than its diff:
```python
import functools

import jax
import jax.numpy as jnp
from jax import lax
from jax.experimental import pallas as pl
from jax.experimental.pallas import tpu as pltpu
from jax.sharding import PartitionSpec as P

MESH = pl.DeviceIdType.MESH
LANES = 128


def flip(value, mask):
    bit = 1
    while bit <= mask:
        if mask & bit:
            value = value + bit - 2 * bit * (value // bit % 2)
        bit *= 2
    return value


def exchange_kernel(sizes, delta, names, got, got_names, local_sem, z_send, z_recv, x_send, x_recv,
                    y_send, y_recv, relay_send, relay_recv, name_send, name_recv):
    n_expert, n_mp = sizes
    n_dest = n_expert * n_mp
    d = lax.axis_index("dp")
    me = lax.axis_index("expert") * n_mp + lax.axis_index("mp")
    x_dp, y_dp = flip(d, 1), flip(d, 2)

    def column(k):
        g = flip(me, k)
        return g, (d, g // n_mp, g % n_mp)

    x_id = (x_dp, me // n_mp, me % n_mp)
    y_id = (y_dp, me // n_mp, me % n_mp)

    def remote(src, dst, send, recv, device):
        return pltpu.make_async_remote_copy(
            src_ref=src, dst_ref=dst, send_sem=send, recv_sem=recv, device_id=device, device_id_type=MESH
        )

    barrier = pltpu.get_barrier_semaphore()
    for k in range(1, n_dest):
        pl.semaphore_signal(barrier, inc=1, device_id=column(k)[1], device_id_type=MESH)
    pl.semaphore_signal(barrier, inc=1, device_id=x_id, device_id_type=MESH)
    pl.semaphore_signal(barrier, inc=1, device_id=y_id, device_id_type=MESH)
    own = pltpu.make_async_copy(delta.at[me], got.at[d, me], local_sem.at[0])
    own.start()
    own_names = pltpu.make_async_copy(names, got_names.at[d, me], local_sem.at[1])
    own_names.start()
    pl.semaphore_wait(barrier, n_dest + 1)

    sent = []
    to_x, to_y = [], []

    def to_neighbours(k):
        g = column(k)[0]
        src = delta.at[me] if k == 0 else got.at[d, g]
        for copies, send, recv, device in ((to_x, x_send, x_recv, x_id), (to_y, y_send, y_recv, y_id)):
            copy = remote(src, got.at[d, g], send.at[k], recv.at[k], device)
            copy.start()
            copies.append(copy)
            sent.append(copy)

    name_copies = []
    for k in range(1, n_dest):
        copy = remote(names, got_names.at[d, me], name_send.at[k], name_recv.at[k], column(k)[1])
        copy.start()
        name_copies.append(copy)
    sent.extend(name_copies)
    to_neighbours(0)
    z_copies = [None]
    for k in range(1, n_dest):
        g, device = column(k)
        copy = remote(delta.at[g], got.at[d, me], z_send.at[k], z_recv.at[k], device)
        copy.start()
        z_copies.append(copy)
        sent.append(copy)

    relays = []

    def relay(k):
        g = column(k)[0]
        if k % 2 == 0:
            to_x[k].wait_recv()
            part, device = got.at[x_dp, g], y_id
        else:
            to_y[k].wait_recv()
            part, device = got.at[y_dp, g], x_id
        copy = remote(part, part, relay_send.at[k], relay_recv.at[k], device)
        copy.start()
        relays.append(copy)
        sent.append(copy)

    lag = 2
    name_x = name_y = None
    for k in range(1, n_dest + lag):
        if k < n_dest:
            z_copies[k].wait_recv()
            to_neighbours(k)
        if k == 2:
            for copy in name_copies:
                copy.wait_recv()
            own_names.wait()
            mine = got_names.at[d]
            name_x = remote(mine, mine, name_send.at[n_dest], name_recv.at[n_dest], x_id)
            name_x.start()
            name_y = remote(mine, mine, name_send.at[n_dest + 1], name_recv.at[n_dest + 1], y_id)
            name_y.start()
        if k >= lag:
            relay(k - lag)
    name_x.wait_recv()
    theirs = got_names.at[x_dp]
    name_relay = remote(theirs, theirs, name_send.at[0], name_recv.at[0], y_id)
    name_relay.start()
    sent.extend([name_x, name_y, name_relay])

    for k in range(n_dest):
        (to_y if k % 2 == 0 else to_x)[k].wait_recv()
    for copy in relays:
        copy.wait_recv()
    name_y.wait_recv()
    name_relay.wait_recv()
    own.wait()
    for copy in sent:
        copy.wait_send()


def exchange(delta, names, sizes, n_dp):
    n_dest = delta.shape[0]
    moved = n_dp * delta.size * 2
    vmem = pl.BlockSpec(memory_space=pltpu.VMEM)
    dma = pltpu.SemaphoreType.DMA
    return pl.pallas_call(
        functools.partial(exchange_kernel, sizes),
        out_shape=(
            jax.ShapeDtypeStruct((n_dp,) + delta.shape, delta.dtype),
            jax.ShapeDtypeStruct((n_dp, n_dest) + names.shape, names.dtype),
        ),
        in_specs=[vmem, vmem],
        out_specs=(vmem, vmem),
        scratch_shapes=[dma((2,))] + [dma((n_dest,))] * 8 + [dma((n_dest + 2,))] * 2,
        compiler_params=pltpu.CompilerParams(
            collective_id=0, has_side_effects=True, vmem_limit_bytes=moved + moved // 4 + 4 * 1024 * 1024
        ),
        cost_estimate=pl.CostEstimate(flops=0, bytes_accessed=32 * moved, transcendentals=0),
    )(delta, names)


def apply_kernel(grid, names, got, base, out, table, listed, total, patch, base_sem, patch_sem):
    row_blocks, col_blocks, pieces = grid
    sources, capacity, size = got.shape[0], got.shape[1], got.shape[2]
    experts, rows, _ = base.shape
    me = lax.axis_index("expert") * lax.axis_size("mp") + lax.axis_index("mp")
    step = rows // pieces

    def base_copy(i):
        part = (i // pieces, pl.ds(i % pieces * step, step))
        return pltpu.make_async_copy(base.at[part], out.at[part], base_sem.at[i])

    for i in range(experts * pieces):
        base_copy(i).start()

    def clear(i, carry):
        table[i] = 0
        return carry

    lax.fori_loop(0, table.shape[0], clear, 0, unroll=16)

    def place(name):
        column = pl.multiple_of(name % col_blocks * size, size)
        row = pl.multiple_of(name // col_blocks % row_blocks * size, size)
        return name // (col_blocks * row_blocks), pl.ds(row, size), pl.ds(column, size)

    def add(slot, count):
        source, k = slot // capacity, slot % capacity
        name = names[source, me * capacity + k]
        live = name >= 0
        seen = table[jnp.maximum(name, 0)]
        fresh = jnp.logical_and(live, seen == 0)

        @pl.when(fresh)
        def _():
            table[name] = count + 1
            listed[count] = name
            total[count] = base[place(name)].astype(jnp.float32) + got[source, k].astype(jnp.float32)

        @pl.when(jnp.logical_and(live, seen > 0))
        def _():
            total[seen - 1] += got[source, k].astype(jnp.float32)

        return count + fresh.astype(jnp.int32)

    count = lax.fori_loop(0, sources * capacity, add, jnp.int32(0))

    def round_once(i, carry):
        patch[i] = total[i].astype(patch.dtype)
        return carry

    lax.fori_loop(0, count, round_once, 0)
    for i in range(experts * pieces):
        base_copy(i).wait()

    def patch_copy(i):
        return pltpu.make_async_copy(patch.at[i], out.at[place(listed[i])], patch_sem.at[i])

    def start(i, carry):
        patch_copy(i).start()
        return carry

    def finish(i, carry):
        patch_copy(i).wait()
        return carry

    lax.fori_loop(0, count, start, 0)
    lax.fori_loop(0, count, finish, 0)


def apply(names, got, base, row_blocks, col_blocks):
    experts = base.shape[0]
    size = got.shape[-1]
    blocks = experts * row_blocks * col_blocks
    most = min(blocks, got.shape[0] * got.shape[1])
    pieces = 4
    vmem = pl.BlockSpec(memory_space=pltpu.VMEM)
    return pl.pallas_call(
        functools.partial(apply_kernel, (row_blocks, col_blocks, pieces)),
        out_shape=jax.ShapeDtypeStruct(base.shape, base.dtype),
        in_specs=[pl.BlockSpec(memory_space=pltpu.SMEM), vmem, vmem],
        out_specs=pl.BlockSpec(memory_space=pl.ANY),
        scratch_shapes=[
            pltpu.SMEM((blocks,), jnp.int32),
            pltpu.SMEM((most,), jnp.int32),
            pltpu.VMEM((most, size, size), jnp.float32),
            pltpu.VMEM((most, size, size), base.dtype),
            pltpu.SemaphoreType.DMA((experts * pieces,)),
            pltpu.SemaphoreType.DMA((most,)),
        ],
        compiler_params=pltpu.CompilerParams(
            vmem_limit_bytes=base.size * 2 + got.size * 2 + most * size * size * 6 + 4 * 1024 * 1024
        ),
        cost_estimate=pl.CostEstimate(flops=0, bytes_accessed=base.size * 4, transcendentals=0),
    )(names, got, base)


def body(base_weights, delta_blocks, block_ids, block_counts, owner_map):
    exp_dev, row_count, col_count = base_weights.shape
    size = delta_blocks.shape[1]
    row_blocks, col_blocks = row_count // size, col_count // size
    n_dp, n_expert, n_mp = lax.axis_size("dp"), lax.axis_size("expert"), lax.axis_size("mp")
    n_dest = n_expert * n_mp
    col_total = col_blocks * n_mp
    slots = delta_blocks.shape[0]
    capacity = slots // n_dest
    active = jnp.arange(slots, dtype=jnp.int32) % capacity < jnp.repeat(block_counts, capacity)
    expert = block_ids // (row_blocks * col_total)
    row_index = block_ids // col_total % row_blocks
    matches = expert[:, None] == jnp.arange(owner_map.shape[0], dtype=jnp.int32)[None, :]
    position = jnp.sum(jnp.where(matches, owner_map[None, :], 0), axis=1)
    idents = (position % exp_dev * row_blocks + row_index) * col_blocks + block_ids % col_blocks
    idents = jnp.where(active, idents, -1)
    width = -(-slots // LANES) * LANES
    names = jnp.pad(idents, (0, width - slots), constant_values=-1).reshape(1, width)
    blocks = delta_blocks.reshape(n_dest, capacity, size, size)
    got, got_names = exchange(blocks, names, (n_expert, n_mp), n_dp)
    return apply(
        got_names.reshape(n_dp * n_dest, width),
        got.reshape(n_dp * n_dest, capacity, size, size),
        base_weights, row_blocks, col_blocks,
    )


def solution(mesh):
    in_specs = (
        P("expert", None, "mp"),
        P(("dp", "expert", "mp"), None, None),
        P(("dp", "expert", "mp")),
        P(("dp", "expert", "mp")),
        P(),
    )
    out_specs = P("expert", None, "mp")
    return jax.shard_map(body, mesh=mesh, in_specs=in_specs, out_specs=out_specs, check_vma=False)
```

time: 220 us -> 48.6 us (0.22); the launches traced: 217 us -> 48.3 us
  local copies, waits for them, and re-layouts: 128 us -> 7.31 us
  other arithmetic: 42.4 us -> 2.09 us
  Pallas kernels: 0 us -> 38.9 us
  blocking collectives: 28.8 us -> 0 us
  between operations: 14 us -> 0.03 us
  starting transfers between devices: 3.34 us -> 0 us
    pallas_call x0 -> x2, Pallas kernels: none -> 38.9 us  [the longest x1 31 us: exchange(): pl.pallas_call(functools.partial(exchange_kernel, sizes), out_shape=(jax....]
    reshape x1, local copies, waits for them, and re-layouts: 35.5 us -> 0.01 us  [body(): jnp.pad(idents, (0, width - slots), constant_values=-1).reshape(1, width)]
    transpose x1 -> x0, local copies, waits for them, and re-layouts: 34.3 us -> none  [to_matrix(): grid.transpose(0, 1, 3, 2, 4)]
    convert_element_type x2 -> x0, other arithmetic: 24.7 us -> none  [the longest x1 20.7 us: body(): return (base_weights.astype(jnp.float32) + task_delta).astype(jnp.bfloat16)]
    all_to_all x1 -> x0, blocking collectives: 21.6 us -> none  [body(): lax.all_to_all(values, ('expert', 'mp'), split_axis=0, concat_axis=0, til...]
    convert_element_type x1 -> x0, local copies, waits for them, and re-layouts: 20.6 us -> none  [body(): return (base_weights.astype(jnp.float32) + task_delta).astype(jnp.bfloat16)]
    unnamed x6 -> x4, local copies, waits for them, and re-layouts: 21.5 us -> 6.5 us
    broadcast_in_dim x1 -> x0, local copies, waits for them, and re-layouts: 14.4 us -> none  [body(): jnp.zeros((exp_dev * row_blocks * col_blocks, block_size, block_size), jn...]
  transfers between devices with their start and end apart: 2 -> 0, of which waited for: 0 -> 0; matrix products, arithmetic and copies ran while one was open for 12% -> 0% of each run, Pallas kernels for 0% -> 0%
where the time goes in v1:
time: 48.6 us; the launch traced here: 48.3 us
  Pallas kernels  38.9 us (80%)
  local copies, waits for them, and re-layouts  7.31 us (15%)
  other arithmetic  2.09 us (4%)
    pallas_call x1, Pallas kernels, exchange(): pl.pallas_call(functools.partial(exchange_kernel, sizes), out_shape=(jax....  31 us
    pallas_call x1, Pallas kernels, apply(): pl.pallas_call(functools.partial(apply_kernel, (row_blocks, col_blocks, p...  7.92 us
    unnamed x4, local copies, waits for them, and re-layouts  6.5 us

profile of v1, /device:TPU:0, one launch (start us, length us, event | category | flops | bytes accessed | tf_op | source)
XLA Modules:
  0.0 48.3 jit_solution(6163698915795465944)
XLA Ops:
  0.0 0.7 %and_select_fusion.4 = s32[16]{0:T(128)S(1)} fusion(s32[16]{0:T(128)} %param.7), kind=kLoop, calls=%fused_computation.8 | loop fusion | flops 128 | bytes 128 | tf_op jit(solution)/shard_map/jit(floor_divide)/jit(_where)/select_n | solution.py:257
  0.7 0.7 %select_reduce_fusion = s32[16]{0:T(128)S(1)} fusion(s32[8]{0:T(128)} %param.9, s32[16]{0:T(128)S(1)} %and_select_fusion.4), kind=kLoop, calls=%fused_computation | loop fusion | flops 368 | bytes 160 | tf_op jit(solution)/shard_map/reduce_sum | solution.py:260
  1.4 0.7 %broadcast_in_dim.20 = s32[8,2]{1,0:T(8,128)S(1)} broadcast(s32[8]{0:T(128)} %param.8), dimensions={0} | broadcast | bytes 96 | tf_op jit(solution)/shard_map/broadcast_in_dim | solution.py:256
  2.1 0.1 reshape.18
  2.2 0.7 %compare_select_fusion.2 = s32[16]{0:T(128)S(1)} fusion(s32[16]{0:T(128)S(1)} %reshape.18, s32[16]{0:T(128)} %param.7, s32[16]{0:T(128)S(1)} %select_reduce_fusion), kind=kLoop, calls=%fused_computation.9 | loop fusion | flops 688 | bytes 256 | tf_op jit(solution)/shard_map/jit(_where)/select_n | solution.py:262
  2.9 0.0 copy-start.1
  2.9 1.0 %copy-done.1 = bf16[16,128,128]{2,1,0:T(8,128)(2,1)S(1)} copy-done((bf16[16,128,128]{2,1,0:T(8,128)(2,1)S(1)}, bf16[16,128,128]{2,1,0:T(8,128)(2,1)}, u32[]{:S(2)}) %copy-start.1) | copy-done | bytes 524312
  3.9 31.0 %shard_map.55 = (bf16[4,8,2,128,128]{4,3,2,1,0:T(8,128)(2,1)S(1)}, s32[4,8,1,128]{3,2,1,0:T(1,128)S(1)}) custom-call(bf16[8,2,128,128]{3,2,1,0:T(8,128)(2,1)S(1)} %bitcast.6, s32[1,128]{1,0:T(1,128)S(1)} %pad_bitcast_fusion.names), custom_call_target="tpu_custom_call" | custom-call | bytes 67108864 | tf_op jit(solution)/shard_map/pallas_call | solution.py:135
  34.9 0.0 copy-start
  35.0 5.5 %copy-done = bf16[2,2560,1536]{2,1,0:T(8,128)(2,1)S(1)} copy-done((bf16[2,2560,1536]{2,1,0:T(8,128)(2,1)S(1)}, bf16[2,2560,1536]{2,1,0:T(8,128)(2,1)}, u32[]{:S(2)}) %copy-start) | copy-done | bytes 15728664
  40.4 7.9 %shard_map.56 = bf16[2,2560,1536]{2,1,0:T(8,128)(2,1)} custom-call(s32[32,128]{1,0:T(8,128)S(1)} %bitcast.7, bf16[32,2,128,128]{3,2,1,0:T(8,128)(2,1)S(1)} %bitcast.5, bf16[2,2560,1536]{2,1,0:T(8,128)(2,1)S(1)} %copy-done), custom_call_target="tpu_custom_call" | custom-call | bytes 31457280 | tf_op jit(solution)/shard_map/pallas_call | solution.py:227
  (1 shorter events, 0.0 us)
Async XLA Ops:
  2.9 1.0 %copy-start.1 = (bf16[16,128,128]{2,1,0:T(8,128)(2,1)S(1)}, bf16[16,128,128]{2,1,0:T(8,128)(2,1)}, u32[]{:S(2)}) copy-start(bf16[16,128,128]{2,1,0:T(8,128)(2,1)} %param.6) | copy-start | bytes 1572868
  34.9 5.5 %copy-start = (bf16[2,2560,1536]{2,1,0:T(8,128)(2,1)S(1)}, bf16[2,2560,1536]{2,1,0:T(8,128)(2,1)}, u32[]{:S(2)}) copy-start(bf16[2,2560,1536]{2,1,0:T(8,128)(2,1)} %base.1) | copy-start | bytes 47185924

commit v2 on v1

v2 whole, which is shorter than its diff:
```python
import functools

import jax
import jax.numpy as jnp
from jax import lax
from jax.experimental import pallas as pl
from jax.experimental.pallas import tpu as pltpu
from jax.sharding import PartitionSpec as P

MESH = pl.DeviceIdType.MESH
VMEM = 67043328
SLACK = 1024 * 1024


def flip(value, mask):
    bit = 1
    while bit <= mask:
        if mask & bit:
            value = value + bit - 2 * bit * (value // bit % 2)
        bit *= 2
    return value


def exchange_kernel(sizes, delta_in, ids_in, counts_in, owners, base_in, got, names, got_counts, base,
                    delta, own_ids, own_counts, got_ids, local_sem, base_sem, z_send, z_recv,
                    x_send, x_recv, y_send, y_recv, relay_send, relay_recv, ids_send, ids_recv,
                    counts_send, counts_recv):
    n_expert, n_mp, row_blocks, col_blocks = sizes
    n_dest = n_expert * n_mp
    d = lax.axis_index("dp")
    me = lax.axis_index("expert") * n_mp + lax.axis_index("mp")
    x_dp, y_dp = flip(d, 1), flip(d, 2)

    def column(k):
        g = flip(me, k)
        return g, (d, g // n_mp, g % n_mp)

    x_id = (x_dp, me // n_mp, me % n_mp)
    y_id = (y_dp, me // n_mp, me % n_mp)

    def remote(src, dst, send, recv, device):
        return pltpu.make_async_remote_copy(
            src_ref=src, dst_ref=dst, send_sem=send, recv_sem=recv, device_id=device, device_id_type=MESH
        )

    barrier = pltpu.get_barrier_semaphore()
    for k in range(1, n_dest):
        pl.semaphore_signal(barrier, inc=1, device_id=column(k)[1], device_id_type=MESH)
    pl.semaphore_signal(barrier, inc=1, device_id=x_id, device_id_type=MESH)
    pl.semaphore_signal(barrier, inc=1, device_id=y_id, device_id_type=MESH)
    early = [
        pltpu.make_async_copy(delta_in, delta, local_sem.at[0]),
        pltpu.make_async_copy(ids_in, own_ids, local_sem.at[1]),
        pltpu.make_async_copy(counts_in, own_counts, local_sem.at[2]),
    ]
    late = [
        pltpu.make_async_copy(delta_in.at[me], got.at[d, me], local_sem.at[3]),
        pltpu.make_async_copy(ids_in, got_ids.at[d, me], local_sem.at[4]),
        pltpu.make_async_copy(counts_in, got_counts.at[d, me], local_sem.at[5]),
    ]
    for copy in early + late:
        copy.start()
    for copy in early:
        copy.wait()
    pl.semaphore_wait(barrier, n_dest + 1)

    sent = []
    to_x, to_y = [], []

    def to_neighbours(k):
        g = column(k)[0]
        src = delta.at[me] if k == 0 else got.at[d, g]
        for copies, send, recv, device in ((to_x, x_send, x_recv, x_id), (to_y, y_send, y_recv, y_id)):
            copy = remote(src, got.at[d, g], send.at[k], recv.at[k], device)
            copy.start()
            copies.append(copy)
            sent.append(copy)

    small = ((own_ids, got_ids, ids_send, ids_recv), (own_counts, got_counts, counts_send, counts_recv))
    small_z, small_x, small_y, small_relay = [], [], [], []
    for k in range(1, n_dest):
        for own, all_of, send, recv in small:
            copy = remote(own, all_of.at[d, me], send.at[k], recv.at[k], column(k)[1])
            copy.start()
            small_z.append(copy)
    to_neighbours(0)
    z_copies = [None]
    for k in range(1, n_dest):
        g, device = column(k)
        copy = remote(delta.at[g], got.at[d, me], z_send.at[k], z_recv.at[k], device)
        copy.start()
        z_copies.append(copy)
        sent.append(copy)
    base_copies = [
        pltpu.make_async_copy(base_in.at[i], base.at[i], base_sem.at[i]) for i in range(base.shape[0])
    ]
    for copy in base_copies:
        copy.start()

    relays = []

    def relay(k):
        g = column(k)[0]
        if k % 2 == 0:
            to_x[k].wait_recv()
            part, device = got.at[x_dp, g], y_id
        else:
            to_y[k].wait_recv()
            part, device = got.at[y_dp, g], x_id
        copy = remote(part, part, relay_send.at[k], relay_recv.at[k], device)
        copy.start()
        relays.append(copy)
        sent.append(copy)

    lag = 2
    for k in range(1, n_dest + lag):
        if k < n_dest:
            z_copies[k].wait_recv()
            to_neighbours(k)
        if k == 2:
            for copy in small_z:
                copy.wait_recv()
            for copy in late[1:]:
                copy.wait()
            for own, all_of, send, recv in small:
                for copies, at, device in ((small_x, n_dest, x_id), (small_y, n_dest + 1, y_id)):
                    copy = remote(all_of.at[d], all_of.at[d], send.at[at], recv.at[at], device)
                    copy.start()
                    copies.append(copy)
        if k >= lag:
            relay(k - lag)
        if k == n_dest - 1:
            for (own, all_of, send, recv), arrived in zip(small, small_x):
                arrived.wait_recv()
                copy = remote(all_of.at[x_dp], all_of.at[x_dp], send.at[0], recv.at[0], y_id)
                copy.start()
                small_relay.append(copy)
    for copy in small_y + small_relay:
        copy.wait_recv()

    per_expert = row_blocks * col_blocks * n_mp
    exp_dev = base.shape[0]

    def whole_quotient(value, divisor):
        return ((value.astype(jnp.float32) + 0.5) * (1.0 / divisor)).astype(jnp.int32)

    def decode(i, carry):
        ids = got_ids[i // n_dest, i % n_dest]
        expert = whole_quotient(ids, per_expert)
        row = whole_quotient(ids, col_blocks * n_mp)
        column_block = ids - row * (col_blocks * n_mp)
        column_block -= whole_quotient(column_block, col_blocks) * col_blocks
        row -= expert * row_blocks
        place = jnp.zeros_like(ids)
        for e in range(owners.shape[0]):
            place = jnp.where(expert == e, owners[e], place)
        place -= whole_quotient(place, exp_dev) * exp_dev
        names[i // n_dest, i % n_dest] = (place * row_blocks + row) * col_blocks + column_block
        return carry

    lax.fori_loop(0, got_ids.shape[0] * n_dest, decode, 0)

    for k in range(n_dest):
        (to_y if k % 2 == 0 else to_x)[k].wait_recv()
    for copy in relays:
        copy.wait_recv()
    late[0].wait()
    for copy in base_copies:
        copy.wait()
    for copy in sent + small_z + small_x + small_y + small_relay:
        copy.wait_send()


def exchange(delta, ids, counts, owners, base, sizes, n_dp):
    n_dest = delta.shape[0]
    moved = n_dp * delta.size * 2
    vmem = pl.BlockSpec(memory_space=pltpu.VMEM)
    hbm = pl.BlockSpec(memory_space=pl.ANY)
    dma = pltpu.SemaphoreType.DMA
    return pl.pallas_call(
        functools.partial(exchange_kernel, sizes),
        out_shape=(
            pltpu.VMEM((n_dp,) + delta.shape, delta.dtype),
            pltpu.VMEM((n_dp, n_dest) + ids.shape, ids.dtype),
            pltpu.VMEM((n_dp, n_dest) + counts.shape, counts.dtype),
            pltpu.VMEM(base.shape, base.dtype),
        ),
        in_specs=[hbm, hbm, hbm, pl.BlockSpec(memory_space=pltpu.SMEM), hbm],
        out_specs=(vmem, vmem, vmem, vmem),
        scratch_shapes=[
            pltpu.VMEM(delta.shape, delta.dtype),
            pltpu.VMEM(ids.shape, ids.dtype),
            pltpu.VMEM(counts.shape, counts.dtype),
            pltpu.VMEM((n_dp, n_dest) + ids.shape, ids.dtype),
            dma((6,)),
            dma((base.shape[0],)),
        ] + [dma((n_dest,))] * 8 + [dma((n_dest + 2,))] * 4,
        compiler_params=pltpu.CompilerParams(
            collective_id=0, has_side_effects=True, vmem_limit_bytes=VMEM - moved - base.size * 2 - SLACK
        ),
        cost_estimate=pl.CostEstimate(flops=0, bytes_accessed=32 * moved, transcendentals=0),
    )(delta, ids, counts, owners, base)


def apply_kernel(grid, names, counts, got, base_in, out, base, table, link, listed, listed_count, patch,
                 base_sem, patch_sem):
    row_blocks, col_blocks, pieces = grid
    sources, capacity, size = got.shape[0], got.shape[1], got.shape[2]
    experts, rows, _ = base.shape
    per_expert = row_blocks * col_blocks
    most = patch.shape[0]
    me = lax.axis_index("expert") * lax.axis_size("mp") + lax.axis_index("mp")
    step = rows // pieces
    split = experts // 2
    scale = -(-(1 << 16) // col_blocks)
    assert per_expert * (scale * col_blocks - (1 << 16)) < 1 << 16

    def base_copy(e, i):
        part = (e, pl.ds(i * step, step))
        return pltpu.make_async_copy(base.at[part], out.at[part], base_sem.at[e * pieces + i])

    def each_base_copy(first, last, action):
        for e in range(first, last):
            for i in range(pieces):
                action(base_copy(e, i))

    each_base_copy(0, split, lambda copy: copy.start())

    def clear(i, carry):
        table[i] = 0
        return carry

    lax.fori_loop(0, table.shape[0], clear, 0, unroll=16)
    for e in range(experts):
        listed_count[e] = 0

    def enter(slot, source, k):
        name = names[source, 0, me * capacity + k]

        @pl.when(k < counts[source, 0, me])
        def _():
            before = table[name]
            table[name] = slot + 1
            link[slot] = before

            @pl.when(before == 0)
            def _():
                e = jnp.int32(0)
                for other in range(1, experts):
                    e += (name >= other * per_expert).astype(jnp.int32)
                count = listed_count[e]
                listed[e * most + count] = name
                listed_count[e] = count + 1

    def enter_source(source, carry):
        for k in range(capacity):
            enter(source * capacity + k, source, k)
        return carry

    lax.fori_loop(0, sources, enter_source, 0)

    def place(e, name):
        rest = name - e * per_expert
        row = lax.shift_right_logical(rest * scale, 16)
        column = rest - row * col_blocks
        return (
            e,
            pl.ds(pl.multiple_of(row * size, size), size),
            pl.ds(pl.multiple_of(column * size, size), size),
        )

    def block_of(slot):
        return got[slot // capacity, slot % capacity].astype(jnp.float32)

    def summed(name, spot):
        head = table[name] - 1
        total = base[spot].astype(jnp.float32) + block_of(head)
        _, total = lax.while_loop(
            lambda state: state[0] > 0,
            lambda state: (link[state[0] - 1], state[1] + block_of(state[0] - 1)),
            (link[head], total),
        )
        return total.astype(base.dtype)

    for e in range(split, experts):
        def in_place(i, carry, e=e):
            name = listed[e * most + i]
            spot = place(e, name)
            base[spot] = summed(name, spot)
            return carry

        lax.fori_loop(0, listed_count[e], in_place, 0)
    each_base_copy(split, experts, lambda copy: copy.start())

    def patch_copy(e, i, at):
        return pltpu.make_async_copy(patch.at[at], out.at[place(e, listed[e * most + i])], patch_sem.at[at])

    first = jnp.int32(0)
    starts = []
    for e in range(split):
        starts.append(first)

        def aside(i, carry, e=e, first=first):
            name = listed[e * most + i]
            patch[first + i] = summed(name, place(e, name))
            return carry

        lax.fori_loop(0, listed_count[e], aside, 0)
        first = first + listed_count[e]
    each_base_copy(0, split, lambda copy: copy.wait())
    for e, first in enumerate(starts):
        def start(i, carry, e=e, first=first):
            patch_copy(e, i, first + i).start()
            return carry

        lax.fori_loop(0, listed_count[e], start, 0)
    each_base_copy(split, experts, lambda copy: copy.wait())
    for e, first in enumerate(starts):
        def finish(i, carry, e=e, first=first):
            patch_copy(e, i, first + i).wait()
            return carry

        lax.fori_loop(0, listed_count[e], finish, 0)


def apply(names, counts, got, base, row_blocks, col_blocks):
    experts = base.shape[0]
    size = got.shape[-1]
    blocks = experts * row_blocks * col_blocks
    slots = got.shape[0] * got.shape[1]
    most = min(blocks, slots)
    pieces = 4
    vmem = pl.BlockSpec(memory_space=pltpu.VMEM)
    smem = pl.BlockSpec(memory_space=pltpu.SMEM)
    out, _ = pl.pallas_call(
        functools.partial(apply_kernel, (row_blocks, col_blocks, pieces)),
        out_shape=(
            jax.ShapeDtypeStruct(base.shape, base.dtype),
            jax.ShapeDtypeStruct(base.shape, base.dtype),
        ),
        in_specs=[smem, smem, vmem, vmem],
        out_specs=(pl.BlockSpec(memory_space=pl.ANY), vmem),
        input_output_aliases={3: 1},
        scratch_shapes=[
            pltpu.SMEM((blocks,), jnp.int32),
            pltpu.SMEM((slots,), jnp.int32),
            pltpu.SMEM((experts * most,), jnp.int32),
            pltpu.SMEM((experts,), jnp.int32),
            pltpu.VMEM((most, size, size), base.dtype),
            pltpu.SemaphoreType.DMA((experts * pieces,)),
            pltpu.SemaphoreType.DMA((most,)),
        ],
        compiler_params=pltpu.CompilerParams(vmem_limit_bytes=most * size * size * 2 + 4 * 1024 * 1024),
        cost_estimate=pl.CostEstimate(flops=0, bytes_accessed=base.size * 4, transcendentals=0),
    )(names, counts, got, base)
    return out


def body(base_weights, delta_blocks, block_ids, block_counts, owner_map):
    exp_dev, row_count, col_count = base_weights.shape
    size = delta_blocks.shape[1]
    row_blocks, col_blocks = row_count // size, col_count // size
    n_dp, n_expert, n_mp = lax.axis_size("dp"), lax.axis_size("expert"), lax.axis_size("mp")
    n_dest = n_expert * n_mp
    slots = delta_blocks.shape[0]
    capacity = slots // n_dest
    assert owner_map.shape[0] * row_blocks * col_blocks * n_mp < 1 << 20
    sources = n_dp * n_dest
    got, names, counts, base = exchange(
        delta_blocks.reshape(n_dest, capacity, size, size),
        block_ids.reshape(1, slots),
        block_counts.reshape(1, n_dest),
        owner_map, base_weights, (n_expert, n_mp, row_blocks, col_blocks), n_dp,
    )
    return apply(
        names.reshape(sources, 1, slots),
        counts.reshape(sources, 1, n_dest),
        got.reshape(sources, capacity, size, size),
        base, row_blocks, col_blocks,
    )


def solution(mesh):
    in_specs = (
        P("expert", None, "mp"),
        P(("dp", "expert", "mp"), None, None),
        P(("dp", "expert", "mp")),
        P(("dp", "expert", "mp")),
        P(),
    )
    out_specs = P("expert", None, "mp")
    return jax.shard_map(body, mesh=mesh, in_specs=in_specs, out_specs=out_specs, check_vma=False)
```

time: 48.6 us -> 39.9 us (0.82)
  local copies, waits for them, and re-layouts: 7.31 us -> 0 us
  other arithmetic: 2.09 us -> 0 us
  Pallas kernels: 38.9 us -> 39.8 us
    unnamed x4 -> x0, local copies, waits for them, and re-layouts: 6.5 us -> none
    pallas_call x1, Pallas kernels: 31 us -> 32.4 us  [exchange(): pl.pallas_call(functools.partial(exchange_kernel, sizes), out_shape=(pltp...]
    select_n x2 -> x0, other arithmetic: 1.35 us -> none  [the longest x1 0.68 us: body(): idents = jnp.where(active, idents, -1)]
    reduce_sum x1 -> x0, other arithmetic: 0.74 us -> none  [body(): position = jnp.sum(jnp.where(matches, owner_map[None, :], 0), axis=1)]
    broadcast_in_dim x1 -> x0, local copies, waits for them, and re-layouts: 0.72 us -> none  [body(): jnp.repeat(block_counts, capacity)]
    pallas_call x1, Pallas kernels: 7.92 us -> 7.37 us  [apply(): pl.pallas_call(functools.partial(apply_kernel, (row_blocks, col_blocks, p...]
where the time goes in v2:
time: 39.9 us; the launch traced here: 39.8 us
  Pallas kernels  39.8 us (100%)
    pallas_call x1, Pallas kernels, exchange(): pl.pallas_call(functools.partial(exchange_kernel, sizes), out_shape=(pltp...  32.4 us
    pallas_call x1, Pallas kernels, apply(): pl.pallas_call(functools.partial(apply_kernel, (row_blocks, col_blocks, p...  7.37 us

profile of v2, /device:TPU:0, one launch (start us, length us, event | category | flops | bytes accessed | tf_op | source)
XLA Modules:
  0.0 39.8 jit_solution(2967030801442989125)
XLA Ops:
  0.0 32.4 %shard_map.55 = (bf16[4,8,2,128,128]{4,3,2,1,0:T(8,128)(2,1)S(1)}, s32[4,8,1,16]{3,2,1,0:T(1,128)S(1)}, s32[4,8,1,8]{3,2,1,0:T(1,128)S(1)}, bf16[2,2560,1536]{2,1,0:T(8,128)(2,1)S(1)}) custom-call(bf16[8,2,128,128]{3,2,1,0:T(8,128)(2,1)} %bitcast.9, s32[1,16]{1,0:T(1,128)} %bitcast.10, s32[1,8]{1,0:T(1,128)} %bitcast.11, s32[8]{0:T(128)} %owners.1, ...), custom_call_target="tpu_custom_call" | custom-call | bytes 67108864 | tf_op jit(solution)/shard_map/pallas_call | solution.py:180
  32.4 7.4 %shard_map.56 = (bf16[2,2560,1536]{2,1,0:T(8,128)(2,1)}, bf16[2,2560,1536]{2,1,0:T(8,128)(2,1)S(1)}) custom-call(s32[32,1,16]{2,1,0:T(1,128)S(1)} %bitcast.7, s32[32,1,8]{2,1,0:T(1,128)S(1)} %bitcast.8, bf16[32,2,128,128]{3,2,1,0:T(8,128)(2,1)S(1)} %bitcast.6, bf16[2,2560,1536]{2,1,0:T(8,128)(2,1)S(1)} %get-tuple-element.13.base_in), custom_call_target="tpu_custom_call", output_to_operand_aliasing={{1}: (3, {})} | custom-call | bytes 31457280 | tf_op jit(solution)/shard_map/pallas_call | solution.py:335

commit v3 on v2

--- a/solution.py
+++ b/solution.py
@@ -202,64 +202,62 @@
     )(delta, ids, counts, owners, base)
 
 
-def apply_kernel(grid, names, counts, got, base_in, out, base, table, link, listed, listed_count, patch,
-                 base_sem, patch_sem):
-    row_blocks, col_blocks, pieces = grid
+def apply_kernel(grid, names_in, counts_in, got, base_in, out, base, names, counts, table, link, listed,
+                 listed_inside, patch, base_sem, patch_sem, local_sem):
+    row_blocks, col_blocks, pieces, beside = grid
     sources, capacity, size = got.shape[0], got.shape[1], got.shape[2]
     experts, rows, _ = base.shape
     per_expert = row_blocks * col_blocks
-    most = patch.shape[0]
     me = lax.axis_index("expert") * lax.axis_size("mp") + lax.axis_index("mp")
     step = rows // pieces
-    split = experts // 2
+    border = beside * (row_blocks // pieces) * col_blocks
     scale = -(-(1 << 16) // col_blocks)
     assert per_expert * (scale * col_blocks - (1 << 16)) < 1 << 16
 
-    def base_copy(e, i):
-        part = (e, pl.ds(i * step, step))
-        return pltpu.make_async_copy(base.at[part], out.at[part], base_sem.at[e * pieces + i])
-
-    def each_base_copy(first, last, action):
-        for e in range(first, last):
-            for i in range(pieces):
-                action(base_copy(e, i))
-
-    each_base_copy(0, split, lambda copy: copy.start())
+    def base_copy(i):
+        part = (i // pieces, pl.ds(i % pieces * step, step))
+        return pltpu.make_async_copy(base.at[part], out.at[part], base_sem.at[i])
+
+    to_smem = [
+        pltpu.make_async_copy(names_in, names, local_sem.at[0]),
+        pltpu.make_async_copy(counts_in, counts, local_sem.at[1]),
+    ]
+    for copy in to_smem:
+        copy.start()
+    for i in range(beside):
+        base_copy(i).start()
 
     def clear(i, carry):
         table[i] = 0
         return carry
 
     lax.fori_loop(0, table.shape[0], clear, 0, unroll=16)
-    for e in range(experts):
-        listed_count[e] = 0
-
-    def enter(slot, source, k):
-        name = names[source, 0, me * capacity + k]
-
-        @pl.when(k < counts[source, 0, me])
-        def _():
+    for copy in to_smem:
+        copy.wait()
+
+    def enter_source(source, carry):
+        outside, inside = carry
+        used = counts[source, 0, me]
+        for k in range(capacity):
+            slot = source * capacity + k
+            name = names[source, 0, me * capacity + k]
+            live = k < used
             before = table[name]
-            table[name] = slot + 1
             link[slot] = before
-
-            @pl.when(before == 0)
-            def _():
-                e = jnp.int32(0)
-                for other in range(1, experts):
-                    e += (name >= other * per_expert).astype(jnp.int32)
-                count = listed_count[e]
-                listed[e * most + count] = name
-                listed_count[e] = count + 1
-
-    def enter_source(source, carry):
-        for k in range(capacity):
-            enter(source * capacity + k, source, k)
-        return carry
-
-    lax.fori_loop(0, sources, enter_source, 0)
-
-    def place(e, name):
+            table[name] = jnp.where(live, slot + 1, before)
+            listed[outside] = name
+            listed_inside[inside] = name
+            fresh = jnp.logical_and(live, before == 0).astype(jnp.int32)
+            first_part = (name < border).astype(jnp.int32)
+            outside, inside = outside + fresh * first_part, inside + fresh * (1 - first_part)
+        return outside, inside
+
+    outside, inside = lax.fori_loop(0, sources, enter_source, (jnp.int32(0), jnp.int32(0)))
+
+    def place(name):
+        e = jnp.int32(0)
+        for other in range(1, experts):
+            e += (name >= other * per_expert).astype(jnp.int32)
         rest = name - e * per_expert
         row = lax.shift_right_logical(rest * scale, 16)
         column = rest - row * col_blocks
@@ -282,45 +280,38 @@
         )
         return total.astype(base.dtype)
 
-    for e in range(split, experts):
-        def in_place(i, carry, e=e):
-            name = listed[e * most + i]
-            spot = place(e, name)
-            base[spot] = summed(name, spot)
-            return carry
-
-        lax.fori_loop(0, listed_count[e], in_place, 0)
-    each_base_copy(split, experts, lambda copy: copy.start())
-
-    def patch_copy(e, i, at):
-        return pltpu.make_async_copy(patch.at[at], out.at[place(e, listed[e * most + i])], patch_sem.at[at])
-
-    first = jnp.int32(0)
-    starts = []
-    for e in range(split):
-        starts.append(first)
-
-        def aside(i, carry, e=e, first=first):
-            name = listed[e * most + i]
-            patch[first + i] = summed(name, place(e, name))
-            return carry
-
-        lax.fori_loop(0, listed_count[e], aside, 0)
-        first = first + listed_count[e]
-    each_base_copy(0, split, lambda copy: copy.wait())
-    for e, first in enumerate(starts):
-        def start(i, carry, e=e, first=first):
-            patch_copy(e, i, first + i).start()
-            return carry
-
-        lax.fori_loop(0, listed_count[e], start, 0)
-    each_base_copy(split, experts, lambda copy: copy.wait())
-    for e, first in enumerate(starts):
-        def finish(i, carry, e=e, first=first):
-            patch_copy(e, i, first + i).wait()
-            return carry
-
-        lax.fori_loop(0, listed_count[e], finish, 0)
+    def in_place(i, carry):
+        spot = place(listed_inside[i])
+        base[spot] = summed(listed_inside[i], spot)
+        return carry
+
+    lax.fori_loop(0, inside, in_place, 0)
+    for i in range(beside, experts * pieces):
+        base_copy(i).start()
+
+    def aside(i, carry):
+        patch[i] = summed(listed[i], place(listed[i]))
+        return carry
+
+    lax.fori_loop(0, outside, aside, 0)
+    for i in range(beside):
+        base_copy(i).wait()
+
+    def patch_copy(i):
+        return pltpu.make_async_copy(patch.at[i], out.at[place(listed[i])], patch_sem.at[i])
+
+    def start(i, carry):
+        patch_copy(i).start()
+        return carry
+
+    def finish(i, carry):
+        patch_copy(i).wait()
+        return carry
+
+    lax.fori_loop(0, outside, start, 0)
+    for i in range(beside, experts * pieces):
+        base_copy(i).wait()
+    lax.fori_loop(0, outside, finish, 0)
 
 
 def apply(names, counts, got, base, row_blocks, col_blocks):
@@ -329,26 +320,29 @@
     blocks = experts * row_blocks * col_blocks
     slots = got.shape[0] * got.shape[1]
     most = min(blocks, slots)
-    pieces = 4
+    pieces = 4 if row_blocks % 4 == 0 else 1
+    beside = experts * pieces * 5 // 8
     vmem = pl.BlockSpec(memory_space=pltpu.VMEM)
-    smem = pl.BlockSpec(memory_space=pltpu.SMEM)
     out, _ = pl.pallas_call(
-        functools.partial(apply_kernel, (row_blocks, col_blocks, pieces)),
+        functools.partial(apply_kernel, (row_blocks, col_blocks, pieces, beside)),
         out_shape=(
             jax.ShapeDtypeStruct(base.shape, base.dtype),
             jax.ShapeDtypeStruct(base.shape, base.dtype),
         ),
-        in_specs=[smem, smem, vmem, vmem],
+        in_specs=[vmem, vmem, vmem, vmem],
         out_specs=(pl.BlockSpec(memory_space=pl.ANY), vmem),
         input_output_aliases={3: 1},
         scratch_shapes=[
+            pltpu.SMEM(names.shape, jnp.int32),
+            pltpu.SMEM(counts.shape, jnp.int32),
             pltpu.SMEM((blocks,), jnp.int32),
             pltpu.SMEM((slots,), jnp.int32),
-            pltpu.SMEM((experts * most,), jnp.int32),
-            pltpu.SMEM((experts,), jnp.int32),
+            pltpu.SMEM((most + 1,), jnp.int32),
+            pltpu.SMEM((most + 1,), jnp.int32),
             pltpu.VMEM((most, size, size), base.dtype),
             pltpu.SemaphoreType.DMA((experts * pieces,)),
             pltpu.SemaphoreType.DMA((most,)),
+            pltpu.SemaphoreType.DMA((2,)),
         ],
         compiler_params=pltpu.CompilerParams(vmem_limit_bytes=most * size * size * 2 + 4 * 1024 * 1024),
         cost_estimate=pl.CostEstimate(flops=0, bytes_accessed=base.size * 4, transcendentals=0),

time: 39.9 us -> 38.9 us (0.975)
  Pallas kernels: 39.8 us -> 38.7 us
    pallas_call x1, Pallas kernels: 7.37 us -> 6.35 us  [apply(): pl.pallas_call(functools.partial(apply_kernel, (row_blocks, col_blocks, p...]
where the time goes in v3:
time: 38.9 us; the launch traced here: 38.7 us
  Pallas kernels  38.7 us (99%)
    pallas_call x1, Pallas kernels, exchange(): pl.pallas_call(functools.partial(exchange_kernel, sizes), out_shape=(pltp...  32.4 us
    pallas_call x1, Pallas kernels, apply(): pl.pallas_call(functools.partial(apply_kernel, (row_blocks, col_blocks, p...  6.35 us

profile of v3, /device:TPU:0, one launch (start us, length us, event | category | flops | bytes accessed | tf_op | source)
XLA Modules:
  0.0 38.7 jit_solution(4893432388865754515)
XLA Ops:
  0.0 32.4 %shard_map.55 = (bf16[4,8,2,128,128]{4,3,2,1,0:T(8,128)(2,1)S(1)}, s32[4,8,1,16]{3,2,1,0:T(1,128)S(1)}, s32[4,8,1,8]{3,2,1,0:T(1,128)S(1)}, bf16[2,2560,1536]{2,1,0:T(8,128)(2,1)S(1)}) custom-call(bf16[8,2,128,128]{3,2,1,0:T(8,128)(2,1)} %bitcast.9, s32[1,16]{1,0:T(1,128)} %bitcast.10, s32[1,8]{1,0:T(1,128)} %bitcast.11, s32[8]{0:T(128)} %owners.1, ...), custom_call_target="tpu_custom_call" | custom-call | bytes 67108864 | tf_op jit(solution)/shard_map/pallas_call | solution.py:180
  32.4 6.3 %shard_map.56 = (bf16[2,2560,1536]{2,1,0:T(8,128)(2,1)}, bf16[2,2560,1536]{2,1,0:T(8,128)(2,1)S(1)}) custom-call(s32[32,1,16]{2,1,0:T(1,128)S(1)} %bitcast.7, s32[32,1,8]{2,1,0:T(1,128)S(1)} %bitcast.8, bf16[32,2,128,128]{3,2,1,0:T(8,128)(2,1)S(1)} %bitcast.6, bf16[2,2560,1536]{2,1,0:T(8,128)(2,1)S(1)} %get-tuple-element.13.base_in), custom_call_target="tpu_custom_call", output_to_operand_aliasing={{1}: (3, {})} | custom-call | bytes 31457280 | tf_op jit(solution)/shard_map/pallas_call | solution.py:326
